TPU v7x, 32 devices: a whole 2x2x4 slice. The times are simulated.
32 devices in a mesh: seq: 16 (over z, y, core), dp: 2 (over x).
Axes of the slice: x: 2, y: 2, z: 4, core: 2. Of those that a mesh axis runs over, the one named last changes fastest.
Arguments:
- q_student: bfloat16 [2, 8192, 1536], P('dp', 'seq'), may hold values from -8 to 8
- kv_student: bfloat16 [2, 128, 3072], P('dp', 'seq'), may hold values from -8 to 8
- q_target: bfloat16 [2, 8192, 1536], P('dp', 'seq'), may hold values from -8 to 8
- kv_target: bfloat16 [2, 128, 3072], P('dp', 'seq'), may hold values from -8 to 8
Outputs:
- student_out: bfloat16 [2, 8192, 1536], P('dp', 'seq')
- target_out: bfloat16 [2, 8192, 1536], P('dp', 'seq')
- distill_loss: float32 [], replicated
All inputs are finite; a program needn't handle non-finite values.
Results may differ from a plain program's by a relative error of at most 0.004.
Values may be sent and summed in bfloat16 or wider, within the bound.
A program may use at most 128 MiB of HBM per device.

v0:
```python
import jax
import jax.numpy as jnp
from jax import lax
from jax.sharding import PartitionSpec as P

HEADS = 12
HD = 128


def absorb(query3, carried, incoming):
    running_max, running_sum, running_out = carried
    block_pairs = incoming[0]
    key_rows = block_pairs.shape[0]
    feature_width = HEADS * HD
    key_block = block_pairs[:, :feature_width].reshape(key_rows, HEADS, HD)
    value_block = block_pairs[:, feature_width:].reshape(key_rows, HEADS, HD)
    scores = jnp.einsum("qhd,khd->hqk", query3, key_block, preferred_element_type=jnp.float32) * (
        1.0 / HD**0.5
    )
    new_max = jnp.maximum(running_max, jnp.max(scores, axis=-1))
    shrink = jnp.exp(running_max - new_max)
    exponent = jnp.exp(scores - new_max[:, :, None])
    running_sum = jnp.sum(exponent, axis=-1)
    running_out = jnp.einsum(
        "hqk,khd->hqd",
        exponent.astype(jnp.bfloat16),
        value_block,
        preferred_element_type=jnp.float32,
    )
    return (new_max, running_sum, running_out)


def normalize(carried, query_rows):
    running_max, running_sum, running_out = carried
    mixed_rows = running_out / running_sum[:, :, None]
    return jnp.transpose(mixed_rows, (1, 0, 2)).reshape(query_rows, HEADS * HD)


def body(q_student, kv_student, q_target, kv_target):
    query_rows = q_student.shape[1]
    student_query = q_student[0].reshape(query_rows, HEADS, HD)
    target_query = q_target[0].reshape(query_rows, HEADS, HD)
    initial = (
        jnp.full((HEADS, query_rows), -1e30, jnp.float32),
        jnp.zeros((HEADS, query_rows), jnp.float32),
        jnp.zeros((HEADS, query_rows, HD), jnp.float32),
    )
    student_all = lax.all_gather(kv_student, "seq", axis=1, tiled=True)
    target_all = lax.all_gather(kv_target, "seq", axis=1, tiled=True)
    student_carry = absorb(student_query, initial, student_all)
    target_carry = absorb(target_query, initial, target_all)
    student_rows = normalize(student_carry, query_rows)
    target_rows = normalize(target_carry, query_rows)
    seq_count = lax.axis_size("seq")
    all_tokens = query_rows * seq_count
    position = (lax.axis_index("seq") * query_rows + jnp.arange(query_rows)).astype(jnp.float32)
    weight = 1.0 + 2.0 * position / float(max(all_tokens - 1, 1))
    gap_rows = student_rows - target_rows
    local_term = jnp.sum(weight[:, None] * gap_rows * gap_rows) / float(all_tokens * HEADS * HD)
    clip_term = lax.psum(local_term, "seq")
    distill_loss = lax.psum(clip_term, "dp")
    return (
        student_rows[None].astype(jnp.bfloat16),
        target_rows[None].astype(jnp.bfloat16),
        distill_loss,
    )


def solution(mesh):
    return jax.shard_map(
        body,
        mesh=mesh,
        in_specs=(
            P("dp", "seq", None),
            P("dp", "seq", None),
            P("dp", "seq", None),
            P("dp", "seq", None),
        ),
        out_specs=(P("dp", "seq", None), P("dp", "seq", None), P()),
        check_vma=False,
    )
```

profile of v0, /device:TPU:0, one launch (start us, length us, event | category | flops | bytes accessed | tf_op | source)
XLA Modules:
  0.0 106.9 jit_solution(2824079883674600560)
XLA Ops:
  0.6 0.0 copy-start
  0.6 25.9 %all_gather.7 = bf16[1,128,3072]{2,1,0:T(8,128)(2,1)S(1)} all-gather(bf16[1,8,3072]{2,1,0:T(8,128)(2,1)} %param.7), channel_id=1, replica_groups=mesh['seq'=16,'dp'=2] {'seq'}, dimensions={1}, use_global_device_ids=true | all-gather | bytes 835584 | tf_op jit(solution)/shard_map/all_gather | solution.py:49
  26.5 0.4 copy.33
  26.9 0.8 fusion.13
  27.7 0.0 copy-done
  27.7 0.7 copy.32
  28.4 0.0 copy-start.4
  28.4 0.6 multiply_reduce_fusion
  29.1 0.6 fusion.3
  29.6 0.0 copy-done.4
  29.6 0.0 copy-start.6
  29.6 2.5 %bitcast_divide_fusion = f32[512,12,128]{0,2,1:T(8,128)} fusion(bf16[128,12,128]{0,2,1:T(8,128)(2,1)S(1)} %bitcast.31, f32[12,512,128]{1,2,0:T(8,128)S(1)} %get-tuple-element.22, f32[512,12]{0,1:T(8,128)S(1)} %bitcast.33, f32[12,512]{1,0:T(8,128)S(1)} %broadcast_maximum_fusion), kind=kOutput, calls=%fused_computation.2 | convolution fusion | flops 204472320 | bytes 6733824 | tf_op jit(solution)/shard_map/hqk,khd->hqd/dot_general | solution.py:24
  32.2 0.0 copy-done.6
  32.2 0.0 copy-start.1
  32.2 19.7 %all_gather.6 = bf16[1,128,3072]{2,1,0:T(8,128)(2,1)S(1)} all-gather(bf16[1,8,3072]{2,1,0:T(8,128)(2,1)S(1)} %copy-done.6), channel_id=1, replica_groups=mesh['seq'=16,'dp'=2] {'seq'}, dimensions={1}, use_global_device_ids=true | all-gather | bytes 835584 | tf_op jit(solution)/shard_map/all_gather | solution.py:48
  51.9 0.4 copy.28
  52.3 0.8 fusion.14
  53.1 0.0 copy-done.1
  53.1 1.6 %copy.27 = bf16[1,512,1536]{1,2,0:T(8,128)(2,1)} copy(bf16[1,512,1536]{2,1,0:T(8,128)(2,1)S(1)} %copy-done.1) | data formatting | bytes 3145728 | tf_op args[0]
  54.7 2.0 %multiply_reduce_fusion.1 = (f32[12,512]{1,0:T(8,128)S(1)}, f32[12,512,128]{1,2,0:T(8,128)S(1)}) fusion(bf16[512,12,128]{0,2,1:T(8,128)(2,1)} %bitcast.23, bf16[128,12,128]{0,2,1:T(8,128)(2,1)S(1)} %bitcast.29), kind=kOutput, calls=%fused_computation.7 | convolution fusion | flops 202893312 | bytes 5136384 | tf_op jit(solution)/shard_map/qhd,khd->hqk/dot_general | solution.py:17
  56.7 0.0 copy-start.3
  56.7 0.0 copy-start.5
  56.7 0.6 copy-done.5
  57.3 1.2 %fusion.1 = f32[12,512]{1,0:T(8,128)} fusion(f32[12,512,128]{1,2,0:T(8,128)S(1)} %get-tuple-element.20, f32[12,512]{1,0:T(8,128)S(1)} %broadcast_maximum_fusion.1), kind=kLoop, calls=%fused_computation.8 | loop fusion | flops 2353152 | bytes 3194880 | tf_op jit(solution)/shard_map/reduce_sum | solution.py:23
  58.5 0.0 copy-done.3
  58.5 6.3 %fusion = (f32[]{:T(128)}, bf16[512,12,128]{0,2,1:T(8,128)(2,1)}, bf16[512,12,128]{0,2,1:T(8,128)(2,1)}) fusion(f32[512,12,128]{0,2,1:T(8,128)} %bitcast_divide_fusion, f32[512]{0:T(512)S(1)} %multiply_add_fusion, f32[512,12]{0,1:T(8,128)} %bitcast.32, bf16[128,12,128]{0,2,1:T(8,128)(2,1)S(1)} %bitcast.30, f32[12,512,128]{1,2,0:T(8,128)S(1)} %get-tuple-element.20, ...), kind=kOutput, calls=%fused_computation.1 | convolution fusion | flops 209190912 | bytes 9881604 | tf_op jit(solution)/shard_map/hqk,khd->hqd/dot_general | solution.py:24
  64.8 0.0 copy-start.2
  64.8 2.7 %copy.37 = bf16[1,512,1536]{2,1,0:T(8,128)(2,1)} copy(bf16[1,512,1536]{1,2,0:T(8,128)(2,1)} %bitcast.27) | data formatting | bytes 3145728
  67.5 0.0 copy-done.2
  67.5 1.6 %copy.38 = bf16[1,512,1536]{2,1,0:T(8,128)(2,1)} copy(bf16[1,512,1536]{1,2,0:T(8,128)(2,1)S(1)} %bitcast.26) | data formatting | bytes 3145728
  69.7 31.7 %psum.14 = f32[]{:T(128)} all-reduce(f32[]{:T(128)S(6)} %div.39), channel_id=1, replica_groups=mesh['seq'=16,'dp'=2] {'seq'}, use_global_device_ids=true, to_apply=%region_5.0 | all-reduce | flops 1 | bytes 8 | tf_op jit(solution)/shard_map/psum | solution.py:60
  101.4 5.5 %psum.15 = f32[]{:T(128)} all-reduce(f32[]{:T(128)} %psum.14), channel_id=1, replica_groups=mesh['seq'=16,'dp'=2] {'dp'}, use_global_device_ids=true, to_apply=%region_6.0 | all-reduce | flops 1 | bytes 8 | tf_op jit(solution)/shard_map/psum | solution.py:61
  (3 shorter events, 0.0 us)
Async XLA Ops:
  0.6 27.1 %copy-start = (bf16[1,512,1536]{2,1,0:T(8,128)(2,1)S(1)}, bf16[1,512,1536]{2,1,0:T(8,128)(2,1)}, u32[]{:S(2)}) copy-start(bf16[1,512,1536]{2,1,0:T(8,128)(2,1)} %param.6) | copy-start | bytes 4718596
  28.4 1.2 %copy-start.4 = (bf16[128,1536]{0,1:T(8,128)(2,1)S(1)}, bf16[128,1536]{0,1:T(8,128)(2,1)}, u32[]{:S(2)}) copy-start(bf16[128,1536]{0,1:T(8,128)(2,1)} %get-tuple-element.16) | copy-start | bytes 1179652
  29.6 2.5 %copy-start.6 = (bf16[1,8,3072]{2,1,0:T(8,128)(2,1)S(1)}, bf16[1,8,3072]{2,1,0:T(8,128)(2,1)}, u32[]{:S(2)}) copy-start(bf16[1,8,3072]{2,1,0:T(8,128)(2,1)} %param.5) | copy-start | bytes 147460
  32.2 20.9 %copy-start.1 = (bf16[1,512,1536]{2,1,0:T(8,128)(2,1)S(1)}, bf16[1,512,1536]{2,1,0:T(8,128)(2,1)}, u32[]{:S(2)}) copy-start(bf16[1,512,1536]{2,1,0:T(8,128)(2,1)} %param.4) | copy-start | bytes 4718596
  56.7 1.8 %copy-start.3 = (bf16[128,1536]{0,1:T(8,128)(2,1)S(1)}, bf16[128,1536]{0,1:T(8,128)(2,1)}, u32[]{:S(2)}) copy-start(bf16[128,1536]{0,1:T(8,128)(2,1)} %get-tuple-element.18) | copy-start | bytes 1179652
  56.7 0.6 copy-start.5
  64.8 2.7 %copy-start.2 = (bf16[512,12,128]{0,2,1:T(8,128)(2,1)S(1)}, bf16[512,12,128]{0,2,1:T(8,128)(2,1)}, u32[]{:S(2)}) copy-start(bf16[512,12,128]{0,2,1:T(8,128)(2,1)} %get-tuple-element.13) | copy-start | bytes 4718596
where the time goes:
time: 107 us
  blocking collectives  82.8 us (77%)
  matrix products  11.5 us (11%)
  local copies, waits for them, and re-layouts  9.49 us (9%)
  other arithmetic  1.75 us (2%)
  between operations  1.39 us (1%)
    psum x1, blocking collectives, body(): clip_term = lax.psum(local_term, 'seq')  31.7 us
    all_gather x1, blocking collectives, body(): target_all = lax.all_gather(kv_target, 'seq', axis=1, tiled=True)  25.9 us
    all_gather x1, blocking collectives, body(): student_all = lax.all_gather(kv_student, 'seq', axis=1, tiled=True)  19.7 us
    dot_general x2, matrix products, absorb(): jnp.einsum('hqk,khd->hqd', exponent.astype(jnp.bfloat16), value_block, pr...  8.79 us
    unnamed x18, local copies, waits for them, and re-layouts  7.15 us
    psum x1, blocking collectives, body(): distill_loss = lax.psum(clip_term, 'dp')  5.54 us
    dot_general x2, matrix products, absorb(): jnp.einsum('qhd,khd->hqk', query3, key_block, preferred_element_type=jnp....  2.66 us

commit v1 on v0

--- a/solution.py
+++ b/solution.py
@@ -58,7 +58,7 @@
     gap_rows = student_rows - target_rows
     local_term = jnp.sum(weight[:, None] * gap_rows * gap_rows) / float(all_tokens * HEADS * HD)
     clip_term = lax.psum(local_term, "seq")
-    distill_loss = lax.psum(clip_term, "dp")
+    distill_loss = jnp.sum(lax.all_gather(clip_term, "dp"), axis=0)
     return (
         student_rows[None].astype(jnp.bfloat16),
         target_rows[None].astype(jnp.bfloat16),

time: 107 us -> 110 us (1.028)
  local copies, waits for them, and re-layouts: 9.49 us -> 11.4 us
    psum x1 -> x0, blocking collectives: 5.54 us -> none  [body(): distill_loss = lax.psum(clip_term, 'dp')]
    unnamed x0 -> x1, blocking collectives: none -> 4.91 us
    unnamed x18 -> x23, local copies, waits for them, and re-layouts: 7.15 us -> 9.02 us
where the time goes in v1:
time: 110 us
  blocking collectives  82.8 us (75%)
  matrix products  11.5 us (10%)
  local copies, waits for them, and re-layouts  11.4 us (10%)
  other arithmetic  2.35 us (2%)
  between operations  1.52 us (1%)
    psum x1, blocking collectives, body(): clip_term = lax.psum(local_term, 'seq')  32.3 us
    all_gather x1, blocking collectives, body(): target_all = lax.all_gather(kv_target, 'seq', axis=1, tiled=True)  25.9 us
    all_gather x1, blocking collectives, body(): student_all = lax.all_gather(kv_student, 'seq', axis=1, tiled=True)  19.7 us
    unnamed x23, local copies, waits for them, and re-layouts  9.02 us
    dot_general x2, matrix products, absorb(): jnp.einsum('hqk,khd->hqd', exponent.astype(jnp.bfloat16), value_block, pr...  8.8 us
    unnamed x1, blocking collectives  4.91 us
    dot_general x2, matrix products, absorb(): jnp.einsum('qhd,khd->hqk', query3, key_block, preferred_element_type=jnp....  2.66 us

profile of v1, /device:TPU:0, one launch (start us, length us, event | category | flops | bytes accessed | tf_op | source)
XLA Modules:
  0.0 109.5 jit_solution(6555222530492951649)
XLA Ops:
  0.6 0.0 copy-start
  0.6 25.9 %all_gather.13 = bf16[1,128,3072]{2,1,0:T(8,128)(2,1)S(1)} all-gather(bf16[1,8,3072]{2,1,0:T(8,128)(2,1)} %param.7), channel_id=1, replica_groups=mesh['seq'=16,'dp'=2] {'seq'}, dimensions={1}, use_global_device_ids=true | all-gather | bytes 835584 | tf_op jit(solution)/shard_map/all_gather | solution.py:49
  26.5 0.4 copy.33
  26.9 0.8 fusion.13
  27.7 0.0 copy-done
  27.7 0.7 copy.32
  28.4 0.0 copy-start.4
  28.4 0.6 multiply_reduce_fusion
  29.1 0.6 fusion.3
  29.6 0.0 copy-done.4
  29.6 0.0 copy-start.6
  29.6 2.5 %bitcast_divide_fusion = f32[512,12,128]{0,2,1:T(8,128)} fusion(bf16[128,12,128]{0,2,1:T(8,128)(2,1)S(1)} %bitcast.33, f32[12,512,128]{1,2,0:T(8,128)S(1)} %get-tuple-element.22, f32[512,12]{0,1:T(8,128)S(1)} %bitcast.35, f32[12,512]{1,0:T(8,128)S(1)} %broadcast_maximum_fusion), kind=kOutput, calls=%fused_computation.2 | convolution fusion | flops 204472320 | bytes 6733824 | tf_op jit(solution)/shard_map/hqk,khd->hqd/dot_general | solution.py:24
  32.2 0.0 copy-done.6
  32.2 0.0 copy-start.1
  32.2 19.7 %all_gather.12 = bf16[1,128,3072]{2,1,0:T(8,128)(2,1)S(1)} all-gather(bf16[1,8,3072]{2,1,0:T(8,128)(2,1)S(1)} %copy-done.6), channel_id=1, replica_groups=mesh['seq'=16,'dp'=2] {'seq'}, dimensions={1}, use_global_device_ids=true | all-gather | bytes 835584 | tf_op jit(solution)/shard_map/all_gather | solution.py:48
  51.9 0.4 copy.28
  52.3 0.8 fusion.14
  53.1 0.0 copy-done.1
  53.1 1.6 %copy.27 = bf16[1,512,1536]{1,2,0:T(8,128)(2,1)} copy(bf16[1,512,1536]{2,1,0:T(8,128)(2,1)S(1)} %copy-done.1) | data formatting | bytes 3145728 | tf_op args[0]
  54.7 2.0 %multiply_reduce_fusion.1 = (f32[12,512]{1,0:T(8,128)S(1)}, f32[12,512,128]{1,2,0:T(8,128)S(1)}) fusion(bf16[512,12,128]{0,2,1:T(8,128)(2,1)} %bitcast.25, bf16[128,12,128]{0,2,1:T(8,128)(2,1)S(1)} %bitcast.31), kind=kOutput, calls=%fused_computation.7 | convolution fusion | flops 202893312 | bytes 5136384 | tf_op jit(solution)/shard_map/qhd,khd->hqk/dot_general | solution.py:17
  56.7 0.0 copy-start.3
  56.7 0.0 copy-start.5
  56.7 0.6 copy-done.5
  57.3 1.2 %fusion.1 = f32[12,512]{1,0:T(8,128)} fusion(f32[12,512,128]{1,2,0:T(8,128)S(1)} %get-tuple-element.20, f32[12,512]{1,0:T(8,128)S(1)} %broadcast_maximum_fusion.1), kind=kLoop, calls=%fused_computation.8 | loop fusion | flops 2353152 | bytes 3194880 | tf_op jit(solution)/shard_map/reduce_sum | solution.py:23
  58.5 0.0 copy-done.3
  58.5 0.0 copy-start.7
  58.5 6.3 %fusion = (f32[]{:T(128)}, bf16[512,12,128]{0,2,1:T(8,128)(2,1)}, bf16[512,12,128]{0,2,1:T(8,128)(2,1)}) fusion(f32[512,12,128]{0,2,1:T(8,128)} %bitcast_divide_fusion, f32[512]{0:T(512)S(1)} %multiply_add_fusion, f32[512,12]{0,1:T(8,128)} %bitcast.34, bf16[128,12,128]{0,2,1:T(8,128)(2,1)S(1)} %bitcast.32, f32[12,512,128]{1,2,0:T(8,128)S(1)} %get-tuple-element.20, ...), kind=kOutput, calls=%fused_computation.1 | convolution fusion | flops 209190912 | bytes 9881604 | tf_op jit(solution)/shard_map/hqk,khd->hqd/dot_general | solution.py:24
  64.8 0.0 copy-start.2
  65.5 32.3 %psum.7 = f32[1]{0:T(128)} all-reduce(f32[1]{0:T(128)} %bitcast.14), channel_id=1, replica_groups=mesh['seq'=16,'dp'=2] {'seq'}, use_global_device_ids=true, to_apply=%region_5.0 | all-reduce | flops 1 | bytes 8 | tf_op jit(solution)/shard_map/psum | solution.py:60
  97.9 0.0 copy-done.7
  97.9 0.6 dynamic-slice
  98.5 1.4 %dynamic-update-slice = f32[2]{0:T(128)S(1)} dynamic-update-slice(f32[2]{0:T(128)S(1)} %broadcast.33, f32[1]{0:T(128)} %psum.7, u32[]{:T(128)} %bitcast.15) | dynamic-update-slice | bytes 12
  99.9 4.9 %all-reduce = f32[2]{0:T(128)S(1)} all-reduce(f32[2]{0:T(128)S(1)} %dynamic-update-slice), channel_id=1, replica_groups=mesh['seq'=16,'dp'=2] {'dp'}, use_global_device_ids=true, to_apply=%add | all-reduce | flops 2 | bytes 16
  104.8 0.6 reduce_sum.39
  105.4 2.6 %copy.37 = bf16[1,512,1536]{2,1,0:T(8,128)(2,1)} copy(bf16[1,512,1536]{1,2,0:T(8,128)(2,1)} %bitcast.29) | data formatting | bytes 3145728
  108.0 0.0 copy-done.2
  108.0 1.6 %copy.38 = bf16[1,512,1536]{2,1,0:T(8,128)(2,1)} copy(bf16[1,512,1536]{1,2,0:T(8,128)(2,1)S(1)} %bitcast.28) | data formatting | bytes 3145728
  (4 shorter events, 0.0 us)
Async XLA Ops:
  0.6 27.1 %copy-start = (bf16[1,512,1536]{2,1,0:T(8,128)(2,1)S(1)}, bf16[1,512,1536]{2,1,0:T(8,128)(2,1)}, u32[]{:S(2)}) copy-start(bf16[1,512,1536]{2,1,0:T(8,128)(2,1)} %param.6) | copy-start | bytes 4718596
  28.4 1.2 %copy-start.4 = (bf16[128,1536]{0,1:T(8,128)(2,1)S(1)}, bf16[128,1536]{0,1:T(8,128)(2,1)}, u32[]{:S(2)}) copy-start(bf16[128,1536]{0,1:T(8,128)(2,1)} %get-tuple-element.16) | copy-start | bytes 1179652
  29.6 2.5 %copy-start.6 = (bf16[1,8,3072]{2,1,0:T(8,128)(2,1)S(1)}, bf16[1,8,3072]{2,1,0:T(8,128)(2,1)}, u32[]{:S(2)}) copy-start(bf16[1,8,3072]{2,1,0:T(8,128)(2,1)} %param.5) | copy-start | bytes 147460
  32.2 20.9 %copy-start.1 = (bf16[1,512,1536]{2,1,0:T(8,128)(2,1)S(1)}, bf16[1,512,1536]{2,1,0:T(8,128)(2,1)}, u32[]{:S(2)}) copy-start(bf16[1,512,1536]{2,1,0:T(8,128)(2,1)} %param.4) | copy-start | bytes 4718596
  56.7 1.8 %copy-start.3 = (bf16[128,1536]{0,1:T(8,128)(2,1)S(1)}, bf16[128,1536]{0,1:T(8,128)(2,1)}, u32[]{:S(2)}) copy-start(bf16[128,1536]{0,1:T(8,128)(2,1)} %get-tuple-element.18) | copy-start | bytes 1179652
  56.7 0.6 copy-start.5
  58.5 39.4 %copy-start.7 = (u32[32]{0:T(128)S(1)}, u32[32]{0:T(128)}, u32[]{:S(2)}) copy-start(u32[32]{0:T(128)} %constant.32) | copy-start | bytes 388
  64.8 43.2 %copy-start.2 = (bf16[512,12,128]{0,2,1:T(8,128)(2,1)S(1)}, bf16[512,12,128]{0,2,1:T(8,128)(2,1)}, u32[]{:S(2)}) copy-start(bf16[512,12,128]{0,2,1:T(8,128)(2,1)} %get-tuple-element.13) | copy-start | bytes 4718596
